TPU v7x, 8 devices: a whole 2x2x1 slice. The times are simulated.
8 devices in a mesh: dp: 2 (over z, y), tp: 4 (over x, core).
Axes of the slice: x: 2, y: 2, z: 1, core: 2. Of those that a mesh axis runs over, the one named last changes fastest.
Arguments:
- hidden: bfloat16 [12, 8, 4096], P('dp'), parts along dimension 0
- draft_ids: int32 [12, 7], P('dp'), parts along dimension 0
- temperature: float32 [12], P('dp'), parts along dimension 0
- norm_gain: bfloat16 [4096], replicated
- head_weight: bfloat16 [128256, 4096], P('tp')
Outputs:
- output 1: float32 [12, 7], P('dp'), parts along dimension 0
- output 2: float32 [12, 8], P('dp'), parts along dimension 0
- output 3: float32 [12, 8], P('dp'), parts along dimension 0
There are 2 independent parts. A program takes and returns all parts, laid end to end along the dimension named above; an argument that names none is the same for every part.
All inputs are finite; a program needn't handle non-finite values.
Results may differ from a plain program's by a relative error of at most 0.001.
Values sent between devices are 32-bit elements.
A program may use at most 1 GiB of HBM per device.

v0:
```python
import jax
import jax.numpy as jnp
from jax import lax
from jax.sharding import PartitionSpec as P, NamedSharding

NORM_EPS = 1e-5


def solution(mesh):
    def local_step(hidden, draft_ids, value_a11, norm_gain, head_shard):
        draft_len = draft_ids.shape[1]
        hidden_f32 = hidden.astype(jnp.float32)
        mean_sq = jnp.mean(hidden_f32 * hidden_f32, axis=-1, keepdims=True)
        normed = (hidden_f32 * lax.rsqrt(mean_sq + NORM_EPS) * norm_gain.astype(jnp.float32)).astype(jnp.bfloat16)
        shard_logits = jnp.einsum("bpd,vd->bpv", normed, head_shard, preferred_element_type=jnp.float32)
        shard_logits = shard_logits / value_a11[:, None, None]
        logits = lax.all_gather(shard_logits, "tp", axis=2, tiled=True)
        row_max = jnp.max(logits, axis=-1, keepdims=True)
        shifted = jnp.exp(logits - row_max)
        total = jnp.sum(shifted, axis=-1)
        weighted = jnp.sum(shifted * logits, axis=-1)
        log_norm = row_max[..., 0] + jnp.log(total)
        entropy = log_norm - weighted / total
        picked = jnp.take_along_axis(logits[:, :draft_len], draft_ids[:, :, None], axis=2)[..., 0]
        return picked - log_norm[:, :draft_len], log_norm, entropy

    return jax.shard_map(
        local_step,
        mesh=mesh,
        in_specs=(P("dp", None, None), P("dp", None), P("dp"), P(None), P("tp", None)),
        out_specs=(P("dp", None), P("dp", None), P("dp", None)),
        check_vma=False,
    )
```

profile of v0, /device:TPU:0, one launch (start us, length us, event | category | flops | bytes accessed | tf_op | source)
XLA Modules:
  0.0 3756.7 jit_solution(8269607315796781923)
XLA Ops:
  7.2 0.0 all-gather.2.cloned.1.call-start
  7.2 0.7 convert_element_type.10
  7.9 1.2 fusion.6
  9.1 94.5 %fusion.3 = f32[6,8,32064]{2,1,0:T(8,128)} fusion(bf16[32064,4096]{1,0:T(8,128)(2,1)} %param.9, f32[6]{0:T(128)} %param.7, bf16[6,8,4096]{2,1,0:T(8,128)(2,1)} %param.5, f32[4096]{0:T(1024)S(1)} %convert_element_type.10, f32[6,8]{1,0:T(8,128)S(1)} %add_rsqrt_fusion), kind=kOutput, calls=%fused_computation.6 | convolution fusion | flops 12610403328 | bytes 269234400 | tf_op jit(solution)/shard_map/bpd,vd->bpv/dot_general | solution.py:15
  103.6 0.0 copy-start.2
  103.6 58.8 %copy.8 = f32[6,8,32064]{1,0,2:T(8,128)} copy(f32[6,8,32064]{2,1,0:T(8,128)} %fusion.3) | data formatting | bytes 12312576 | tf_op jit(solution)/shard_map/div | solution.py:16
  162.4 0.0 all-gather.2.cloned.1.call-update
  162.5 0.0 copy-done.2
  162.5 0.6 reshape.42
  163.1 2992.6 %all-gather.2.cloned.1.call-done = f32[6,8,128256]{1,0,2:T(8,128)} async-done(((f32[6,8,32064]{1,0,2:T(8,128)}), f32[6,8,128256]{1,0,2:T(8,128)}) %all-gather.2.cloned.1.call-update) | async-done | bytes 24625168 | tf_op jit(solution)/shard_map/all_gather | solution.py:17
  3155.7 0.0 copy-start
  3155.7 257.8 %copy.10 = f32[6,7,128256]{2,1,0:T(8,128)} copy(f32[6,7,128256]{1,0,2:T(8,128)} %bitcast.12) | data formatting | bytes 43094016
  3413.6 0.0 copy-done
  3413.6 2.1 gather_fusion
  3415.7 0.7 gather.7
  3416.3 156.8 %reduce_max.9 = f32[6,8]{1,0:T(8,128)S(1)} reduce(f32[6,8,128256]{1,0,2:T(8,128)} %all-gather.2.cloned.1.call-done, f32[]{:T(128)} %constant.24.clone.1), dimensions={2}, to_apply=%region_1.0 | reduce | flops 6156240 | bytes 24625348 | tf_op jit(solution)/shard_map/reduce_max | solution.py:18
  3573.2 0.0 copy-start.3
  3573.2 0.0 copy-start.4
  3573.2 175.5 %multiply_reduce_fusion = (f32[6,8]{1,0:T(8,128)S(1)}, f32[6,8]{1,0:T(8,128)S(1)}) fusion(f32[6,8,128256]{1,0,2:T(8,128)} %all-gather.2.cloned.1.call-done, f32[6,8]{1,0:T(8,128)S(1)} %reduce_max.9), kind=kLoop, calls=%fused_computation.1 | loop fusion | flops 24625056 | bytes 24625728 | tf_op jit(solution)/shard_map/reduce_sum | solution.py:21
  3748.7 0.6 divide_subtract_fusion
  3749.3 0.0 copy-start.1
  3749.3 0.0 copy-done.3
  3749.3 0.0 copy-done.4
  3749.3 0.6 slice_subtract_fusion
  3749.9 0.0 copy-done.1
  (6 shorter events, 0.0 us)
Async XLA Ops:
  7.2 3148.6 %all-gather.2.cloned.1.call-start = ((), (), s32[]{:S(2)}) async-start(), calls=%async_computation | async-start | bytes 656670720 | tf_op jit(solution)/shard_map/all_gather | solution.py:17
  103.6 58.9 %copy-start.2 = (s32[6,7]{1,0:T(8,128)S(1)}, s32[6,7]{1,0:T(8,128)}, u32[]{:S(2)}) copy-start(s32[6,7]{1,0:T(8,128)} %param.6) | copy-start | bytes 508
  3155.7 257.9 %copy-start = (s32[42]{0:T(128)S(1)}, s32[42]{0:T(128)}, u32[]{:S(2)}) copy-start(s32[42]{0:T(128)} %reshape.42) | copy-start | bytes 508
  3573.2 176.1 %copy-start.3 = (s32[6,7]{1,0:T(8,128)S(1)}, s32[6,7]{1,0:T(8,128)}, u32[]{:S(2)}) copy-start(s32[6,7]{1,0:T(8,128)} %param.6) | copy-start | bytes 508
  3573.2 176.1 %copy-start.4 = (f32[6,7]{1,0:T(8,128)S(1)}, f32[6,7]{1,0:T(8,128)}, u32[]{:S(2)}) copy-start(f32[6,7]{1,0:T(8,128)} %gather.7) | copy-start | bytes 508
  3749.3 0.6 copy-start.1
Sparse Core Ops, SparseCore 0:
  162.6 2993.1 all-gather.1
where the time goes:
time: 3760 us
  waiting for transfers between devices  2990 us (80%)
  other arithmetic  335 us (9%)
  local copies, waits for them, and re-layouts  320 us (9%)
  matrix products  94.5 us (3%)
    all_gather x1, waiting for transfers between devices, local_step(): logits = lax.all_gather(shard_logits, 'tp', axis=2, tiled=True)  2990 us
    unnamed x13, local copies, waits for them, and re-layouts  258 us
    reduce_sum x1, other arithmetic, local_step(): weighted = jnp.sum(shifted * logits, axis=-1)  175 us
    reduce_max x1, other arithmetic, local_step(): row_max = jnp.max(logits, axis=-1, keepdims=True)  157 us
    dot_general x1, matrix products, local_step(): jnp.einsum('bpd,vd->bpv', normed, head_shard, preferred_element_type=jnp....  94.5 us
  transfers between devices with their start and end apart: 1, of which 1 were waited for; matrix products, arithmetic and copies ran while one was open for 0% of the time, Pallas kernels for 0%

commit v1 on v0

v1 whole, which is shorter than its diff:
```python
import functools

import jax
import jax.numpy as jnp
from jax import lax
from jax.experimental import pallas as pl
from jax.experimental.pallas import tpu as pltpu
from jax.sharding import PartitionSpec as P

NORM_EPS = 1e-5
LOG2E = 1.4426950408889634
LOWEST = -3.0e38
MESH = pl.DeviceIdType.MESH
TILE = 1024
SLOTS = 6
PRIVATE_TILES = 3
CHUNK = 8


def kernel(
    h_ref, draft_ref, temp_ref, gain_ref, w_ref, lp_ref, lse_ref, ent_ref,
    wbuf, hbuf, gbuf, hsend, hrecv, g, aux, auxin, stats, statsin, draft_s, temp_s,
    wsem, insem, send_sem, recv_sem, fsend_sem, frecv_sem, asem, ssend_sem, srecv_sem,
):
    dp, tp = lax.axis_index("dp"), lax.axis_index("tp")
    core = lax.rem(tp, 2)
    mate = tp + 1 - 2 * core
    rows, dim = w_ref.shape
    tokens = hbuf.shape[0]
    batch, positions = temp_s.shape[1], tokens // temp_s.shape[1]
    shared = (rows - PRIVATE_TILES * TILE) // 2 // TILE * TILE
    private = rows - 2 * shared
    first = private - PRIVATE_TILES * TILE
    total = 1 + PRIVATE_TILES + shared // TILE

    def offset(i):
        return first + (i - 1) * TILE

    def tile_copy(i):
        start = offset(i) + jnp.where(i > PRIVATE_TILES, dp * shared, 0)
        slot = lax.rem(i, SLOTS)
        return pltpu.make_async_copy(
            w_ref.at[pl.ds(pl.multiple_of(start, 64), TILE), :], wbuf.at[slot], wsem.at[slot]
        )

    def first_copy():
        return pltpu.make_async_copy(
            w_ref.at[pl.ds(0, first), :], wbuf.at[0, pl.ds(0, first), :], wsem.at[0]
        )

    inputs = [
        pltpu.make_async_copy(h_ref, hbuf, insem.at[0]),
        pltpu.make_async_copy(gain_ref, gbuf, insem.at[1]),
        pltpu.make_async_copy(draft_ref, draft_s, insem.at[2]),
        pltpu.make_async_copy(temp_ref, temp_s, insem.at[3]),
    ]
    for copy in inputs:
        copy.start()
    first_copy().start(priority=1)
    for i in range(1, SLOTS):
        tile_copy(i).start(priority=1)

    barrier = pltpu.get_barrier_semaphore()
    peers = []
    for j in range(1, 8):
        peer_dp = 1 - dp if j >= 4 else dp
        peer_tp = tp if j % 4 == 0 else (mate if j % 4 == 1 else None)
        if j % 4 == 2:
            peer_tp = lax.rem(tp + 2, 4)
        elif j % 4 == 3:
            peer_tp = lax.rem(mate + 2, 4)
        peers.append((peer_dp, peer_tp))
        pl.semaphore_signal(barrier, inc=1, device_id=(peer_dp, peer_tp), device_id_type=MESH)

    for copy in inputs:
        copy.wait()
    hidden = hbuf[...].astype(jnp.float32)
    hsend[...] = hidden

    lane = lax.broadcasted_iota(jnp.int32, (1, 128), 1)
    inner = lax.rem(lane, 64)
    temp_row = jnp.ones((1, 128), jnp.float32)
    draft_row = jnp.full((1, 128), -1, jnp.int32)
    for b in range(batch):
        temp_row = jnp.where(inner // positions == b, temp_s[0, b], temp_row)
        for p in range(positions - 1):
            draft_row = jnp.where(inner == b * positions + p, draft_s[b, p], draft_row)
    aux[0:1, :] = temp_row
    aux[1:2, :] = draft_row.astype(jnp.float32)
    aux[2:8, :] = jnp.zeros((6, 128), jnp.float32)

    def normed(block, at):
        mean_sq = jnp.mean(block * block, axis=-1, keepdims=True)
        inverse_rms = lax.rsqrt(mean_sq + NORM_EPS)
        gain = gbuf[...].astype(jnp.float32)
        for k in range(dim // 128):
            columns = slice(k * 128, (k + 1) * 128)
            scaled = block[:, columns] * inverse_rms * gain[k:k + 1, :]
            g[at:at + tokens, columns] = scaled.astype(jnp.bfloat16)

    g[...] = jnp.zeros_like(g)
    normed(hidden, 0)

    pl.semaphore_wait(barrier, 7)
    half = tokens // 2
    chunks = half // CHUNK

    def rows_of(which, k):
        return pl.ds(pl.multiple_of(which * half + k * CHUNK, CHUNK), CHUNK)

    def partner_copy(k):
        return pltpu.make_async_remote_copy(
            src_ref=hsend.at[rows_of(core, k), :], dst_ref=hrecv.at[rows_of(core, k), :],
            send_sem=send_sem.at[k], recv_sem=recv_sem.at[k],
            device_id=(1 - dp, tp), device_id_type=MESH,
        )

    def forward_copy(k):
        return pltpu.make_async_remote_copy(
            src_ref=hrecv.at[rows_of(core, k), :], dst_ref=hrecv.at[rows_of(core, k), :],
            send_sem=fsend_sem.at[k], recv_sem=frecv_sem.at[k],
            device_id=(dp, mate), device_id_type=MESH,
        )

    def forwarded_in(k):
        return pltpu.make_async_remote_copy(
            src_ref=hrecv.at[rows_of(1 - core, k), :], dst_ref=hrecv.at[rows_of(1 - core, k), :],
            send_sem=fsend_sem.at[k], recv_sem=frecv_sem.at[k],
            device_id=(dp, mate), device_id_type=MESH,
        )

    aux_copy = pltpu.make_async_remote_copy(
        src_ref=aux, dst_ref=auxin, send_sem=asem.at[0], recv_sem=asem.at[1],
        device_id=(1 - dp, tp), device_id_type=MESH,
    )
    aux_copy.start()
    for k in range(chunks):
        partner_copy(k).start()

    def scored(block, start, carry, scale, draft):
        top, total_exp, weighted, picked = carry
        groups = block.shape[0] // 8
        logits = lax.dot_general(
            block, g[...], (((1,), (1,)), ((), ())), preferred_element_type=jnp.float32
        ).reshape(groups, 8, 128)
        new_top = jnp.maximum(top, jnp.max(logits, axis=0))
        decay = jnp.exp2((top - new_top) * scale)
        shifted = jnp.exp2((logits - new_top[None]) * scale[None])
        total_exp = total_exp * decay + jnp.sum(shifted, axis=0)
        weighted = weighted * decay + jnp.sum(shifted * logits, axis=0)
        row = lax.broadcasted_iota(jnp.int32, (groups, 8, 128), 0) * 8 + lax.broadcasted_iota(
            jnp.int32, (groups, 8, 128), 1
        )
        picked = picked + jnp.sum(jnp.where(row == (draft - start)[None], logits, 0.0), axis=0)
        return new_top, total_exp, weighted, picked

    def body(i, carry, scale, draft):
        tile_copy(i).wait()
        start = tp * rows + offset(i) + jnp.where(i > PRIVATE_TILES, dp * shared, 0)
        carry = scored(wbuf[lax.rem(i, SLOTS)], start, carry, scale, draft)

        @pl.when(i + SLOTS < total)
        def _():
            tile_copy(i + SLOTS).start(priority=1)

        return carry

    zero = jnp.zeros((8, 128), jnp.float32)
    scale = jnp.broadcast_to(LOG2E / temp_row, (8, 128))
    draft = jnp.broadcast_to(draft_row, (8, 128))
    carry = (zero + LOWEST, zero, zero, zero)
    first_copy().wait()
    carry = scored(wbuf[0, 0:first, :], tp * rows, carry, scale, draft)
    tile_copy(SLOTS).start(priority=1)
    for i in range(1, PRIVATE_TILES + 1):
        carry = body(i, carry, scale, draft)
        if i >= 2 and i - 2 < chunks:
            partner_copy(i - 2).wait_recv()
            forward_copy(i - 2).start()

    aux_copy.wait()
    for k in range(chunks):
        if k > PRIVATE_TILES - 2:
            partner_copy(k).wait_recv()
            forward_copy(k).start()
    for k in range(chunks):
        forwarded_in(k).wait_recv()
    normed(hrecv[...], 64)

    own = lax.broadcasted_iota(jnp.int32, (8, 128), 1) < 64
    temp_row = jnp.where(lane < 64, temp_row, auxin[0:1, :])
    draft_row = jnp.where(lane < 64, draft_row, auxin[1:2, :].astype(jnp.int32))
    scale = jnp.broadcast_to(LOG2E / temp_row, (8, 128))
    draft = jnp.broadcast_to(draft_row, (8, 128))
    top, total_exp, weighted, picked = carry
    carry = (
        jnp.where(own, top, LOWEST), jnp.where(own, total_exp, 0.0),
        jnp.where(own, weighted, 0.0), jnp.where(own, picked, 0.0),
    )
    top, total_exp, weighted, picked = lax.fori_loop(
        1 + PRIVATE_TILES, total, functools.partial(body, scale=scale, draft=draft), carry
    )

    best = jnp.max(top, axis=0, keepdims=True)
    decay = jnp.exp2((top - best) * scale)
    stats[0:1, :] = best
    stats[1:2, :] = jnp.sum(total_exp * decay, axis=0, keepdims=True)
    stats[2:3, :] = jnp.sum(weighted * decay, axis=0, keepdims=True)
    stats[3:4, :] = jnp.sum(picked, axis=0, keepdims=True)
    stats[4:8, :] = jnp.zeros((4, 128), jnp.float32)

    def stats_copy(j):
        return pltpu.make_async_remote_copy(
            src_ref=stats, dst_ref=statsin.at[tp + 4 * (j // 4)],
            send_sem=ssend_sem.at[j], recv_sem=srecv_sem.at[j],
            device_id=peers[j - 1], device_id_type=MESH,
        )

    for j in range(1, 8):
        stats_copy(j).start()
    for k in range(chunks):
        partner_copy(k).wait_send()
        forward_copy(k).wait_send()
    statsin[tp] = stats[...]
    for j in range(1, 8):
        stats_copy(j).wait_recv()
    parts = [statsin[j] if j < 4 else pltpu.roll(statsin[j], 64, 1) for j in range(8)]
    best = functools.reduce(jnp.maximum, [part[0:1] for part in parts])
    scale, inverse = scale[0:1], 1.0 / temp_row
    decays = [jnp.exp2((part[0:1] - best) * scale) for part in parts]
    sum_exp = sum(part[1:2] * d for part, d in zip(parts, decays))
    sum_weighted = sum(part[2:3] * d for part, d in zip(parts, decays))
    pick = sum(part[3:4] for part in parts)
    log_norm = best * inverse + jnp.log(sum_exp)

    results = jnp.concatenate([
        pick * inverse - log_norm, log_norm, log_norm - sum_weighted / sum_exp * inverse,
        jnp.zeros((5, 128), jnp.float32),
    ])
    for b in range(batch):
        turned = results if b == 0 else pltpu.roll(results, 128 - b * positions, 1)
        lp_ref[b:b + 1, :] = turned[0:1, 0:positions - 1]
        lse_ref[b:b + 1, :] = turned[1:2, 0:positions]
        ent_ref[b:b + 1, :] = turned[2:3, 0:positions]
    for j in range(1, 8):
        stats_copy(j).wait_send()


def solution(mesh):
    def local_step(hidden, draft_ids, temperature, norm_gain, head_shard):
        batch, positions, dim = hidden.shape
        tokens = batch * positions
        any_spec = pl.BlockSpec(memory_space=pl.ANY)
        chunks = tokens // 2 // CHUNK
        return pl.pallas_call(
            kernel,
            out_shape=(
                jax.ShapeDtypeStruct((batch, positions - 1), jnp.float32),
                jax.ShapeDtypeStruct((batch, positions), jnp.float32),
                jax.ShapeDtypeStruct((batch, positions), jnp.float32),
            ),
            in_specs=[any_spec] * 5,
            out_specs=[pl.BlockSpec(memory_space=pltpu.VMEM)] * 3,
            scratch_shapes=[
                pltpu.VMEM((SLOTS, TILE, dim), jnp.bfloat16),
                pltpu.VMEM((tokens, dim), jnp.bfloat16),
                pltpu.VMEM((dim // 128, 128), jnp.bfloat16),
                pltpu.VMEM((tokens, dim), jnp.float32),
                pltpu.VMEM((tokens, dim), jnp.float32),
                pltpu.VMEM((128, dim), jnp.bfloat16),
                pltpu.VMEM((8, 128), jnp.float32),
                pltpu.VMEM((8, 128), jnp.float32),
                pltpu.VMEM((8, 128), jnp.float32),
                pltpu.VMEM((8, 8, 128), jnp.float32),
                pltpu.SMEM(draft_ids.shape, jnp.int32),
                pltpu.SMEM((1, batch), jnp.float32),
                pltpu.SemaphoreType.DMA((SLOTS,)),
                pltpu.SemaphoreType.DMA((4,)),
                pltpu.SemaphoreType.DMA((chunks,)),
                pltpu.SemaphoreType.DMA((chunks,)),
                pltpu.SemaphoreType.DMA((chunks,)),
                pltpu.SemaphoreType.DMA((chunks,)),
                pltpu.SemaphoreType.DMA((2,)),
                pltpu.SemaphoreType.DMA((8,)),
                pltpu.SemaphoreType.DMA((8,)),
            ],
            compiler_params=pltpu.CompilerParams(
                collective_id=0, has_side_effects=True, vmem_limit_bytes=65_000_000
            ),
            name="score",
        )(hidden.reshape(tokens, dim), draft_ids, temperature.reshape(1, batch), norm_gain.reshape(dim // 128, 128), head_shard)

    return jax.shard_map(
        local_step,
        mesh=mesh,
        in_specs=(P("dp", None, None), P("dp", None), P("dp"), P(None), P("tp", None)),
        out_specs=(P("dp", None), P("dp", None), P("dp", None)),
        check_vma=False,
    )
```

time: 3760 us -> 64.9 us (0.02)
  waiting for transfers between devices: 2990 us -> 0 us
  other arithmetic: 335 us -> 0 us
  local copies, waits for them, and re-layouts: 320 us -> 3.8 us
  matrix products: 94.5 us -> 0 us
  Pallas kernels: 0 us -> 60.2 us
    all_gather x1 -> x0, waiting for transfers between devices: 2990 us -> none  [local_step(): logits = lax.all_gather(shard_logits, 'tp', axis=2, tiled=True)]
    unnamed x13 -> x3, local copies, waits for them, and re-layouts: 258 us -> 3.8 us
    reduce_sum x2 -> x0, other arithmetic: 177 us -> none  [the longest x1 175 us: local_step(): weighted = jnp.sum(shifted * logits, axis=-1)]
    reduce_max x1 -> x0, other arithmetic: 157 us -> none  [local_step(): row_max = jnp.max(logits, axis=-1, keepdims=True)]
    dot_general x1 -> x0, matrix products: 94.5 us -> none  [local_step(): jnp.einsum('bpd,vd->bpv', normed, head_shard, preferred_element_type=jnp....]
    pallas_call x0 -> x1, Pallas kernels: none -> 60.2 us  [local_step(): pl.pallas_call(kernel, out_shape=(jax.ShapeDtypeStruct((batch, positions...]
    div x1 -> x0, local copies, waits for them, and re-layouts: 58.8 us -> none  [local_step(): shard_logits = shard_logits / value_a11[:, None, None]]
  transfers between devices with their start and end apart: 1 -> 0, of which waited for: 1 -> 0; matrix products, arithmetic and copies ran while one was open for 0% -> 0% of each run, Pallas kernels for 0% -> 0%
where the time goes in v1:
time: 64.9 us; the launch traced here: 64.7 us
  Pallas kernels  60.2 us (93%)
  local copies, waits for them, and re-layouts  3.8 us (6%)
    pallas_call x1, Pallas kernels, local_step(): pl.pallas_call(kernel, out_shape=(jax.ShapeDtypeStruct((batch, positions...  60.2 us
    unnamed x3, local copies, waits for them, and re-layouts  3.8 us

profile of v1, /device:TPU:0, one launch (start us, length us, event | category | flops | bytes accessed | tf_op | source)
XLA Modules:
  0.0 64.7 jit_solution(17456986334148238031)
XLA Ops:
  0.6 60.2 %score.1 = (f32[6,7]{1,0:T(8,128)}, f32[6,8]{1,0:T(8,128)}, f32[6,8]{1,0:T(8,128)}) custom-call(bf16[48,4096]{1,0:T(8,128)(2,1)} %bitcast.3, s32[6,7]{1,0:T(8,128)} %draft_ref.1, f32[1,6]{1,0:T(1,128)} %bitcast.5, bf16[32,128]{1,0:T(8,128)(2,1)} %bitcast.4, bf16[32064,4096]{1,0:T(8,128)(2,1)} %w_ref.1), custom_call_target="tpu_custom_call" | custom-call | tf_op jit(solution)/shard_map/score/pallas_call | solution.py:255
  60.9 1.3 %copy.11 = f32[6,7]{1,0:T(8,128)} copy(f32[6,7]{1,0:T(8,128)} %get-tuple-element.6) | data formatting | bytes 336
  62.1 1.3 %copy.12 = f32[6,8]{1,0:T(8,128)} copy(f32[6,8]{1,0:T(8,128)} %get-tuple-element.7) | data formatting | bytes 384
  63.4 1.3 %copy.13 = f32[6,8]{1,0:T(8,128)} copy(f32[6,8]{1,0:T(8,128)} %get-tuple-element.8) | data formatting | bytes 384
